TPU v7x, 32 devices: a whole 2x2x4 slice. The times are simulated.
32 devices in a mesh: dp: 8 (over y, x, core), seq: 4 (over z).
Axes of the slice: x: 2, y: 2, z: 4, core: 2. Of those that a mesh axis runs over, the one named last changes fastest.
Arguments:
- tokens: bfloat16 [16384, 1024], P(('dp', 'seq')), may hold values from -6 to 6
- cotangent: bfloat16 [16384, 1024], P(('dp', 'seq')), may hold values from -6 to 6
- qkv_weight: bfloat16 [1024, 3072], replicated, may hold values from -0.1875 to 0.1875
- proj_weight: bfloat16 [1024, 1024], replicated, may hold values from -0.75 to 0.75
- up_weight: bfloat16 [1024, 4096], replicated, may hold values from -0.1875 to 0.1875
- down_weight: bfloat16 [4096, 1024], replicated, may hold values from -0.09375 to 0.09375
- norm_gains: float32 [2, 1024], replicated, may hold values from 0.5 to 1.5
- biases: float32 [6, 1024], replicated, may hold values from -1.5 to 1.5
- up_bias: float32 [4096], replicated, may hold values from -1.5 to 1.5
- head_slopes: float32 [16], replicated, may hold values from 0.00012207031 to 0.5, as said below
- qkv_moment: float32 [1024, 3072], P(None, 'dp'), may hold values from -1536 to 1536
- proj_moment: float32 [1024, 1024], P(None, 'dp'), may hold values from -1536 to 1536
- up_moment: float32 [1024, 4096], P(None, 'dp'), may hold values from -1536 to 1536
- down_moment: float32 [4096, 1024], P('dp'), may hold values from -1536 to 1536
- gains_moment: float32 [2, 1024], P(None, 'dp'), may hold values from -768 to 768
- biases_moment: float32 [6, 1024], P(None, 'dp'), may hold values from -768 to 768
- upbias_moment: float32 [4096], P('dp'), may hold values from -768 to 768
Outputs:
- block_out: bfloat16 [16384, 1024], P(('dp', 'seq'))
- tokens_grad: float32 [16384, 1024], P(('dp', 'seq'))
- qkv_grad: float32 [1024, 3072], P(None, 'dp')
- proj_grad: float32 [1024, 1024], P(None, 'dp')
- up_grad: float32 [1024, 4096], P(None, 'dp')
- down_grad: float32 [4096, 1024], P('dp')
- gains_grad: float32 [2, 1024], P(None, 'dp')
- biases_grad: float32 [6, 1024], P(None, 'dp')
- upbias_grad: float32 [4096], P('dp')
- qkv_state: float32 [1024, 3072], P(None, 'dp')
- proj_state: float32 [1024, 1024], P(None, 'dp')
- up_state: float32 [1024, 4096], P(None, 'dp')
- down_state: float32 [4096, 1024], P('dp')
- gains_state: float32 [2, 1024], P(None, 'dp')
- biases_state: float32 [6, 1024], P(None, 'dp')
- upbias_state: float32 [4096], P('dp')
- qkv_new: float32 [1024, 3072], P(None, 'dp')
- proj_new: float32 [1024, 1024], P(None, 'dp')
- up_new: float32 [1024, 4096], P(None, 'dp')
- down_new: float32 [4096, 1024], P('dp')
- gains_new: float32 [2, 1024], P(None, 'dp')
- biases_new: float32 [6, 1024], P(None, 'dp')
- upbias_new: float32 [4096], P('dp')
Inputs may be any that keep to these rules, and one draw needn't show every extreme that they name: `head_slopes`: one positive slope a head.
All inputs are finite; a program needn't handle non-finite values.
Results may differ from a plain program's by a relative error of at most 0.025.
Values may be sent and summed in bfloat16 or wider, within the bound.
A program may use at most 256 MiB of HBM per device.

v0:
```python
import math
import jax
import jax.numpy as jnp
from jax import lax
from jax.sharding import PartitionSpec as P

NS_ITERS = 5
MOMENTUM = 0.9
RATE_MATRIX = 0.2
RATE_VECTOR = 0.0015
NORM_EPS = 1e-05
ORTHO_EPS = 1e-07
COEF_A = 2.0
COEF_B = -1.0
GELU_C = 0.7978845608028654
MASKED = -1e30


def norm_forward(values, gain_row, offset):
    center = values - jnp.mean(values, axis=-1, keepdims=True)
    inv_scale = lax.rsqrt(jnp.mean(center * center, axis=-1, keepdims=True) + NORM_EPS)
    unit_values = center * inv_scale
    return (unit_values * gain_row + offset, unit_values, inv_scale)


def norm_backward(upstream, unit_values, inv_scale, gain_row):
    scaled = upstream * gain_row
    inner_sum = jnp.mean(scaled * unit_values, axis=-1, keepdims=True)
    input_grad = inv_scale * (
        scaled - jnp.mean(scaled, axis=-1, keepdims=True) - unit_values * inner_sum
    )
    return (input_grad, jnp.sum(upstream * unit_values, axis=0), jnp.sum(upstream, axis=0))


def gelu_tanh(values):
    return 0.5 * values * (1.0 + jnp.tanh(GELU_C * (values + 0.044715 * values * values * values)))


def gelu_slope(values):
    tangent = jnp.tanh(GELU_C * (values + 0.044715 * values * values * values))
    return 0.5 * (1.0 + tangent) + 0.5 * values * (1.0 - tangent * tangent) * GELU_C * (
        1.0 + 3.0 * 0.044715 * values * values
    )


def contract_rows(left, right):
    return lax.dot_general(
        left, right, (((0,), (0,)), ((), ())), preferred_element_type=jnp.float32
    )


def contract_cols(left, right):
    return lax.dot_general(
        left, right, (((1,), (1,)), ((), ())), preferred_element_type=jnp.float32
    )


def split_heads(matrix, groups):
    row_count = matrix.shape[0]
    return jnp.moveaxis(matrix.reshape(row_count, groups, 2, -1), 1, 0)


def join_heads(stacked):
    row_count = stacked.shape[1]
    return jnp.moveaxis(stacked, 0, 1).reshape(row_count, -1)


def score_block(query_g, key_g, slope_g, distance, allowed):
    scale = 1.0 / math.sqrt(query_g.shape[-1])
    scores = jnp.einsum("qhd,khd->hqk", query_g, key_g, preferred_element_type=jnp.float32) * scale
    scores = scores - slope_g[:, None, None] * distance[None]
    return jnp.where(allowed[None], scores, MASKED)


def group_forward(items, distance, allowed):
    query_g, key_g, value_g, slope_g = items
    scores = score_block(query_g, key_g, slope_g, distance, allowed)
    peak_score = jnp.max(scores, axis=-1, keepdims=True)
    log_total = peak_score + jnp.log(jnp.sum(jnp.exp(scores - peak_score), axis=-1, keepdims=True))
    soft_weights = jnp.exp(scores - log_total).astype(jnp.bfloat16)
    attended = jnp.einsum("hqk,khd->qhd", soft_weights, value_g, preferred_element_type=jnp.float32)
    return (attended, log_total[..., 0])


def group_backward(items, distance, allowed):
    query_g, key_g, value_g, slope_g, log_total, upstream_g = items
    scale = 1.0 / math.sqrt(query_g.shape[-1])
    scores = score_block(query_g, key_g, slope_g, distance, allowed)
    chances = jnp.exp(scores - log_total[..., None])
    soft_weights = chances.astype(jnp.bfloat16)
    soft_grad = jnp.einsum("qhd,khd->hqk", upstream_g, value_g, preferred_element_type=jnp.float32)
    inner_sum = jnp.sum(soft_grad * chances, axis=-1, keepdims=True)
    score_grad = (chances * (soft_grad - inner_sum)).astype(jnp.bfloat16)
    query_grad = (
        jnp.einsum("hqk,khd->qhd", score_grad, key_g, preferred_element_type=jnp.float32) * scale
    ).astype(jnp.bfloat16)
    key_grad = (
        jnp.einsum("hqk,qhd->khd", score_grad, query_g, preferred_element_type=jnp.float32) * scale
    )
    value_grad = jnp.einsum(
        "hqk,qhd->khd", soft_weights, upstream_g, preferred_element_type=jnp.float32
    )
    return (query_grad, key_grad, value_grad)


def on_device(
    tokens,
    cotangent,
    qkv_weight,
    proj_weight,
    up_weight,
    down_weight,
    norm_gains,
    biases,
    up_bias,
    head_slopes,
    qkv_moment,
    proj_moment,
    up_moment,
    down_moment,
    gains_moment,
    biases_moment,
    upbias_moment,
):
    row_count, model_width = tokens.shape
    groups = head_slopes.shape[0] // 2
    seq_length = row_count * lax.axis_size("seq")
    positions = lax.axis_index("seq") * row_count + jnp.arange(row_count, dtype=jnp.int32)
    key_index = jnp.arange(seq_length, dtype=jnp.int32)
    distance = (positions[:, None] - key_index[None, :]).astype(jnp.float32)
    allowed = key_index[None, :] <= positions[:, None]
    slopes = head_slopes.reshape(groups, 2)
    inputs = tokens.astype(jnp.float32)
    normed_one, unit_one, scale_one = norm_forward(inputs, norm_gains[0], biases[0])
    normed_one = normed_one.astype(jnp.bfloat16)
    mixed = jnp.dot(normed_one, qkv_weight, preferred_element_type=jnp.float32)
    queries = (mixed[:, :model_width] + biases[1]).astype(jnp.bfloat16)
    key_part = mixed[:, model_width : 2 * model_width].astype(jnp.bfloat16)
    value_part = (mixed[:, 2 * model_width :] + biases[2]).astype(jnp.bfloat16)
    key_rows, value_rows = (
        lax.all_gather(key_part, "seq", axis=0, tiled=True),
        lax.all_gather(value_part, "seq", axis=0, tiled=True),
    )
    query_groups = split_heads(queries, groups)
    key_groups = split_heads(key_rows, groups)
    value_groups = split_heads(value_rows, groups)

    def forward_group(items):
        return group_forward(items, distance, allowed)

    attended, log_totals = lax.map(forward_group, (query_groups, key_groups, value_groups, slopes))
    mixed_heads = join_heads(attended).astype(jnp.bfloat16)
    middle = (
        inputs + jnp.dot(mixed_heads, proj_weight, preferred_element_type=jnp.float32) + biases[3]
    )
    normed_two, unit_two, scale_two = norm_forward(middle, norm_gains[1], biases[4])
    normed_two = normed_two.astype(jnp.bfloat16)
    before = jnp.dot(normed_two, up_weight, preferred_element_type=jnp.float32) + up_bias
    hidden = gelu_tanh(before).astype(jnp.bfloat16)
    block_out = (
        middle + jnp.dot(hidden, down_weight, preferred_element_type=jnp.float32) + biases[5]
    ).astype(jnp.bfloat16)
    upstream = cotangent.astype(jnp.float32)
    down_grad = contract_rows(cotangent, hidden)
    hidden_grad = contract_cols(cotangent, down_weight)
    before_grad = (hidden_grad * gelu_slope(before)).astype(jnp.bfloat16)
    up_grad = contract_rows(normed_two, before_grad)
    normed_two_grad = contract_cols(before_grad, up_weight)
    middle_back, gain_two_grad, offset_two_grad = norm_backward(
        normed_two_grad, unit_two, scale_two, norm_gains[1]
    )
    middle_grad = upstream + middle_back
    branch_grad = middle_grad.astype(jnp.bfloat16)
    proj_grad = contract_rows(mixed_heads, branch_grad)
    heads_grad = contract_cols(branch_grad, proj_weight).astype(jnp.bfloat16)

    def backward_group(items):
        return group_backward(items, distance, allowed)

    query_grad, key_grad, value_grad = lax.map(
        backward_group,
        (
            query_groups,
            key_groups,
            value_groups,
            slopes,
            log_totals,
            split_heads(heads_grad, groups),
        ),
    )
    query_grad = join_heads(query_grad)
    key_sum, value_sum = (
        lax.psum_scatter(
            join_heads(key_grad).astype(jnp.bfloat16), "seq", scatter_dimension=0, tiled=True
        ).astype(jnp.float32),
        lax.psum_scatter(
            join_heads(value_grad).astype(jnp.bfloat16), "seq", scatter_dimension=0, tiled=True
        ).astype(jnp.float32),
    )
    key_low = key_sum.astype(jnp.bfloat16)
    value_low = value_sum.astype(jnp.bfloat16)
    mixed_grad = jnp.concatenate([query_grad, key_low, value_low], axis=1)
    qkv_grad = contract_rows(normed_one, mixed_grad)
    normed_one_grad = contract_cols(mixed_grad, qkv_weight)
    input_back, gain_one_grad, offset_one_grad = norm_backward(
        normed_one_grad, unit_one, scale_one, norm_gains[0]
    )
    tokens_grad = middle_grad + input_back
    gains_grad = jnp.stack([gain_one_grad, gain_two_grad])
    biases_grad = jnp.stack(
        [
            offset_one_grad,
            jnp.sum(query_grad.astype(jnp.float32), axis=0),
            jnp.sum(value_low.astype(jnp.float32), axis=0),
            jnp.sum(branch_grad.astype(jnp.float32), axis=0),
            offset_two_grad,
            jnp.sum(upstream, axis=0),
        ]
    )
    upbias_grad = jnp.sum(before_grad.astype(jnp.float32), axis=0)[None]
    qkv_part, proj_part, up_part, down_part, gains_part, biases_part, upbias_part = (
        lax.psum_scatter(
            qkv_grad.astype(jnp.bfloat16), "dp", scatter_dimension=1, tiled=True
        ).astype(jnp.float32),
        lax.psum_scatter(
            proj_grad.astype(jnp.bfloat16), "dp", scatter_dimension=1, tiled=True
        ).astype(jnp.float32),
        lax.psum_scatter(
            up_grad.astype(jnp.bfloat16), "dp", scatter_dimension=1, tiled=True
        ).astype(jnp.float32),
        lax.psum_scatter(
            down_grad.astype(jnp.bfloat16), "dp", scatter_dimension=1, tiled=True
        ).astype(jnp.float32),
        lax.psum_scatter(
            gains_grad.astype(jnp.bfloat16), "dp", scatter_dimension=1, tiled=True
        ).astype(jnp.float32),
        lax.psum_scatter(
            biases_grad.astype(jnp.bfloat16), "dp", scatter_dimension=1, tiled=True
        ).astype(jnp.float32),
        lax.psum_scatter(
            upbias_grad.astype(jnp.bfloat16), "dp", scatter_dimension=1, tiled=True
        ).astype(jnp.float32),
    )
    qkv_sum, proj_sum, up_sum, down_sum, gains_sum, biases_sum, upbias_sum = (
        lax.psum(qkv_part.astype(jnp.bfloat16), "seq").astype(jnp.float32),
        lax.psum(proj_part.astype(jnp.bfloat16), "seq").astype(jnp.float32),
        lax.psum(up_part.astype(jnp.bfloat16), "seq").astype(jnp.float32),
        lax.psum(down_part.astype(jnp.bfloat16), "seq").astype(jnp.float32),
        lax.psum(gains_part.astype(jnp.bfloat16), "seq").astype(jnp.float32),
        lax.psum(biases_part.astype(jnp.bfloat16), "seq").astype(jnp.float32),
        lax.psum(upbias_part.astype(jnp.bfloat16), "seq").astype(jnp.float32),
    )
    qkv_state = MOMENTUM * qkv_moment + qkv_sum
    proj_state = MOMENTUM * proj_moment + proj_sum
    up_state = MOMENTUM * up_moment + up_sum
    down_oriented = MOMENTUM * down_moment.T + down_sum
    gains_state = MOMENTUM * gains_moment + gains_sum
    biases_state = MOMENTUM * biases_moment + biases_sum
    upbias_state = MOMENTUM * upbias_moment + upbias_sum[0]
    oriented = (qkv_state, proj_state, up_state, down_oriented)
    pad_width = max((member.shape[1] for member in oriented))
    stacked = jnp.stack(
        [
            jnp.pad(member.astype(jnp.bfloat16), ((0, 0), (0, pad_width - member.shape[1])))
            for member in oriented
        ]
    )
    owned_block = lax.dynamic_index_in_dim(stacked, lax.axis_index("seq"), 0, keepdims=False)
    iterate = owned_block
    for iteration in range(NS_ITERS):
        gram = lax.psum(contract_cols(iterate, iterate).astype(jnp.bfloat16), "dp").astype(
            jnp.float32
        )
        if iteration == 0:
            factor = 1.0 / (jnp.sqrt(jnp.trace(gram)) + ORTHO_EPS)
            square = gram * factor * factor
            iterate = (owned_block.astype(jnp.float32) * factor).astype(jnp.bfloat16)
        else:
            square = gram
        square_low = square.astype(jnp.bfloat16)
        iterate = (
            COEF_A * iterate.astype(jnp.float32)
            + COEF_B * jnp.dot(square_low, iterate, preferred_element_type=jnp.float32)
        ).astype(jnp.bfloat16)
    shared = lax.all_gather(iterate[None], "seq", axis=0, tiled=True)

    def step_of(slot_number, column_count, whole_shape):
        return (
            -RATE_MATRIX
            * math.sqrt(max(whole_shape[0], whole_shape[1]))
            * shared[slot_number][:, :column_count].astype(jnp.float32)
        )

    dp_index = lax.axis_index("dp")

    def own_cols(matrix, count):
        return lax.dynamic_slice_in_dim(matrix, dp_index * count, count, 1).astype(jnp.float32)

    qkv_new = own_cols(qkv_weight, qkv_state.shape[1]) + step_of(
        0, qkv_state.shape[1], qkv_weight.shape
    )
    proj_new = own_cols(proj_weight, proj_state.shape[1]) + step_of(
        1, proj_state.shape[1], proj_weight.shape
    )
    up_new = own_cols(up_weight, up_state.shape[1]) + step_of(2, up_state.shape[1], up_weight.shape)
    down_count = down_oriented.shape[1]
    down_rows = lax.dynamic_slice_in_dim(down_weight, dp_index * down_count, down_count, 0).astype(
        jnp.float32
    )
    down_new = down_rows + step_of(3, down_count, down_weight.shape).T
    gains_new = own_cols(norm_gains, gains_state.shape[1]) - RATE_VECTOR * gains_state
    biases_new = own_cols(biases, biases_state.shape[1]) - RATE_VECTOR * biases_state
    upbias_count = upbias_state.shape[0]
    upbias_new = (
        lax.dynamic_slice_in_dim(up_bias, dp_index * upbias_count, upbias_count, 0)
        - RATE_VECTOR * upbias_state
    )
    return (
        block_out,
        tokens_grad,
        qkv_sum,
        proj_sum,
        up_sum,
        down_sum.T,
        gains_sum,
        biases_sum,
        upbias_sum[0],
        qkv_state,
        proj_state,
        up_state,
        down_oriented.T,
        gains_state,
        biases_state,
        upbias_state,
        qkv_new,
        proj_new,
        up_new,
        down_new,
        gains_new,
        biases_new,
        upbias_new,
    )


def solution(mesh):
    placed = (
        P(("dp", "seq"), None),
        P(("dp", "seq"), None),
        P(),
        P(),
        P(),
        P(),
        P(),
        P(),
        P(),
        P(),
        P(None, "dp"),
        P(None, "dp"),
        P(None, "dp"),
        P("dp", None),
        P(None, "dp"),
        P(None, "dp"),
        P("dp"),
    )
    return jax.shard_map(
        on_device,
        mesh=mesh,
        in_specs=placed,
        out_specs=(
            P(("dp", "seq"), None),
            P(("dp", "seq"), None),
            P(None, "dp"),
            P(None, "dp"),
            P(None, "dp"),
            P("dp", None),
            P(None, "dp"),
            P(None, "dp"),
            P("dp"),
            P(None, "dp"),
            P(None, "dp"),
            P(None, "dp"),
            P("dp", None),
            P(None, "dp"),
            P(None, "dp"),
            P("dp"),
            P(None, "dp"),
            P(None, "dp"),
            P(None, "dp"),
            P("dp", None),
            P(None, "dp"),
            P(None, "dp"),
            P("dp"),
        ),
        check_vma=False,
    )
```

profile of v0, /device:TPU:0, one launch (start us, length us, event | category | flops | bytes accessed | tf_op | source)
XLA Modules:
  0.0 1661.3 jit_solution(17056713743389701598)
XLA Ops:
  12.8 6.1 fusion.105
  26.7 78.8 %all-gather.5.cloned.1.call-done = bf16[2048,1024]{1,0:T(8,128)(2,1)} async-done(((bf16[512,1024]{1,0:T(8,128)(2,1)}), bf16[2048,1024]{1,0:T(8,128)(2,1)}) %all-gather.5.cloned.1.call-update) | async-done | bytes 4194320 | tf_op jit(solution)/shard_map/all_gather | solution.py:142
  105.5 6.5 copy.60
  112.0 74.9 %all-gather.7.cloned.1.call-done = bf16[2048,1024]{1,0:T(8,128)(2,1)} async-done(((bf16[512,1024]{1,0:T(8,128)(2,1)}), bf16[2048,1024]{1,0:T(8,128)(2,1)}) %all-gather.7.cloned.1.call-update) | async-done | bytes 4194320 | tf_op jit(solution)/shard_map/all_gather | solution.py:141
  186.9 6.5 copy.62
  193.4 102.7 %while.30 = (s32[]{:T(128)}, bf16[8,512,2,64]{1,3,2,0:T(8,128)(2,1)}, f32[8,2,512]{2,1,0:T(2,128)S(1)}, bf16[8,2048,2,64]{1,3,2,0:T(8,128)(2,1)}, bf16[8,512,2,6...) while((s32[]{:T(128)}, ...), condition=%wide.region_5.6_spmd.clone.clone, body=%wide.region_2.5_spmd.clone.clone.sunk | while | flops 575667200 | bytes 47618196 | solution.py:151
  201.7 4.5 fusion.167
  214.5 4.5 fusion.167
  220.1 4.0 fusion.166
  227.4 4.5 fusion.167
  240.2 4.5 fusion.167
  253.0 4.5 fusion.167
  265.9 4.5 fusion.167
  278.7 4.5 fusion.167
  291.5 4.5 fusion.167
  299.1 10.7 fusion.107
  309.8 13.6 fusion.113
  323.4 5.7 multiply_reduce_fusion.1
  334.6 222.8 %while.31 = (s32[]{:T(128)}, bf16[8,512,2,64]{1,3,2,0:T(8,128)(2,1)}, bf16[8,2048,2,64]{1,3,2,0:T(8,128)(2,1)}, bf16[8,2048,2,64]{1,3,2,0:T(8,128)(2,1)}, bf16[8...) while((s32[]{:T(128)}, ...), condition=%wide.region_12.13_spmd.clone.clone, body=%wide.region_10.12_spmd.clone.clone.sunk | while | flops 1368783872 | bytes 144864496 | solution.py:180
  343.3 5.7 multiply_reduce_fusion.7
  349.0 6.6 multiply_convert_fusion.7
  371.1 5.7 multiply_reduce_fusion.7
  376.8 6.6 multiply_convert_fusion.7
  391.5 4.0 subtract_exponential_fusion.2
  398.9 5.7 multiply_reduce_fusion.7
  404.6 6.6 multiply_convert_fusion.7
  419.3 4.0 subtract_exponential_fusion.2
  426.7 5.7 multiply_reduce_fusion.7
  432.4 6.6 multiply_convert_fusion.7
  454.5 5.7 multiply_reduce_fusion.7
  460.3 6.6 multiply_convert_fusion.7
  482.4 5.7 multiply_reduce_fusion.7
  488.1 6.6 multiply_convert_fusion.7
  510.2 5.7 multiply_reduce_fusion.7
  515.9 6.6 multiply_convert_fusion.7
  530.6 4.0 subtract_exponential_fusion.2
  538.0 5.7 multiply_reduce_fusion.7
  543.7 6.6 multiply_convert_fusion.7
  561.8 4.3 copy.73
  566.6 66.1 %reduce-scatter.20.cloned.1.call-done = bf16[512,1024]{0,1:T(8,128)(2,1)} async-done(((bf16[2048,1024]{0,1:T(8,128)(2,1)}), bf16[512,1024]{0,1:T(8,128)(2,1)}) %reduce-scatter.20.cloned.1.call-update) | async-done | bytes 1048592 | tf_op jit(solution)/shard_map/reduce_scatter | solution.py:193
  632.7 79.5 %reduce-scatter.22.cloned.1.call-done = bf16[512,1024]{0,1:T(8,128)(2,1)} async-done(((bf16[2048,1024]{0,1:T(8,128)(2,1)}), bf16[512,1024]{0,1:T(8,128)(2,1)}) %reduce-scatter.22.cloned.1.call-update) | async-done | bytes 1048592 | tf_op jit(solution)/shard_map/reduce_scatter | solution.py:196
  712.2 8.1 convolution_convert_fusion.1
  720.3 8.6 copy.71
  730.2 11.4 convert_bitcast_fusion
  743.2 9.2 convolution_convert_fusion
  752.7 4.9 reduce-scatter.30.cloned.1.call-done
  759.4 63.2 %reduce-scatter.28.cloned.1.call-done = bf16[384,1024]{1,0:T(8,128)(2,1)} async-done(((bf16[3072,1024]{1,0:T(8,128)(2,1)}), bf16[384,1024]{1,0:T(8,128)(2,1)}) %reduce-scatter.28.cloned.1.call-update) | async-done | bytes 786448
  824.9 72.5 %reduce-scatter.26.cloned.1.call-done = bf16[1024,512]{1,0:T(8,128)(2,1)} async-done(((bf16[1024,4096]{1,0:T(8,128)(2,1)}), bf16[1024,512]{1,0:T(8,128)(2,1)}) %reduce-scatter.26.cloned.1.call-update) | async-done | bytes 1048592 | tf_op jit(solution)/shard_map/reduce_scatter | solution.py:231
  897.4 74.8 %reduce-scatter.24.cloned.1.call-done = bf16[1024,512]{1,0:T(8,128)(2,1)} async-done(((bf16[1024,4096]{1,0:T(8,128)(2,1)}), bf16[1024,512]{1,0:T(8,128)(2,1)}) %reduce-scatter.24.cloned.1.call-update) | async-done | bytes 1048592 | tf_op jit(solution)/shard_map/reduce_scatter | solution.py:228
  975.1 121.9 %all-reduce.21.cloned.1.call-done = (bf16[1024,384]{1,0:T(8,128)(2,1)}, bf16[1024,128]{1,0:T(8,128)(2,1)}, bf16[1024,512]{1,0:T(8,128)(2,1)}, bf16[1024,512]{1,0:T(8,128)(2,1)}) async-done(((bf16[1024,384]{1,0:T(8,128)(2,1)}, bf16[1024,128]{1,0:T(8,128)(2,1)}, bf16[1024,512]{1,0:T(8,128)(2,1)}, bf16[1024,512]{1,0:T(8,128)(2,1)}), (bf16[1024,384]{1,0:T(8,128)(2,1)}, bf16[1024,128]{1,0:T(8,128)(2,1)}, ...) | async-done | bytes 3145744 | tf_op jit(solution)/shard_map/psum | solution.py:245
  1112.3 60.9 %all-reduce.11.cloned.1.call-done = bf16[1024,1024]{1,0:T(8,128)(2,1)} async-done(((bf16[1024,1024]{1,0:T(8,128)(2,1)}), bf16[1024,1024]{1,0:T(8,128)(2,1)}) %all-reduce.11.cloned.1.call-update) | async-done | bytes 2097168 | tf_op jit(solution)/shard_map/psum | solution.py:271
  1183.4 60.9 %all-reduce.13.cloned.1.call-done = bf16[1024,1024]{1,0:T(8,128)(2,1)} async-done(((bf16[1024,1024]{1,0:T(8,128)(2,1)}), bf16[1024,1024]{1,0:T(8,128)(2,1)}) %all-reduce.13.cloned.1.call-update) | async-done | bytes 2097168 | tf_op jit(solution)/shard_map/psum | solution.py:271
  1251.4 60.9 %all-reduce.15.cloned.1.call-done = bf16[1024,1024]{1,0:T(8,128)(2,1)} async-done(((bf16[1024,1024]{1,0:T(8,128)(2,1)}), bf16[1024,1024]{1,0:T(8,128)(2,1)}) %all-reduce.15.cloned.1.call-update) | async-done | bytes 2097168 | tf_op jit(solution)/shard_map/psum | solution.py:271
  1319.5 60.9 %all-reduce.17.cloned.1.call-done = bf16[1024,1024]{1,0:T(8,128)(2,1)} async-done(((bf16[1024,1024]{1,0:T(8,128)(2,1)}), bf16[1024,1024]{1,0:T(8,128)(2,1)}) %all-reduce.17.cloned.1.call-update) | async-done | bytes 2097168 | tf_op jit(solution)/shard_map/psum | solution.py:271
  1389.4 9.4 fusion.80
  1404.0 44.5 %all-reduce.19.cloned.1.call-done = bf16[1024,1024]{1,0:T(8,128)(2,1)} async-done(((bf16[1024,1024]{1,0:T(8,128)(2,1)}), bf16[1024,1024]{1,0:T(8,128)(2,1)}) %all-reduce.19.cloned.1.call-update) | async-done | bytes 2097168 | tf_op jit(solution)/shard_map/psum | solution.py:271
  1448.5 4.4 add_convert_fusion
  1457.5 12.6 add_convert_fusion.5
  1470.1 17.1 %reduce-scatter.36.cloned.1.call-done = bf16[512,1]{1,0:T(8,128)(2,1)} async-done(((bf16[4096,1]{1,0:T(8,128)(2,1)}), bf16[512,1]{1,0:T(8,128)(2,1)}) %reduce-scatter.36.cloned.1.call-update) | async-done | bytes 1040
  1488.3 4.2 fusion.79
  1492.5 31.8 %reduce-scatter.32.cloned.1.call-done = bf16[128,2]{1,0:T(8,128)(2,1)} async-done(((bf16[1024,2]{1,0:T(8,128)(2,1)}), bf16[128,2]{1,0:T(8,128)(2,1)}) %reduce-scatter.32.cloned.1.call-update) | async-done | bytes 528
  1525.2 35.7 %reduce-scatter.34.cloned.1.call-done = bf16[128,6]{1,0:T(8,128)(2,1)} async-done(((bf16[1024,6]{1,0:T(8,128)(2,1)}), bf16[128,6]{1,0:T(8,128)(2,1)}) %reduce-scatter.34.cloned.1.call-update) | async-done | bytes 1552
  1561.7 11.8 all-reduce.2
  1584.4 58.7 %all-gather.9.cloned.1.call-done = bf16[4096,512]{1,0:T(8,128)(2,1)} async-done(((bf16[1024,512]{1,0:T(8,128)(2,1)}), bf16[4096,512]{1,0:T(8,128)(2,1)}) %all-gather.9.cloned.1.call-update) | async-done | bytes 4194320 | tf_op jit(solution)/shard_map/all_gather | solution.py:285
  (369 shorter events, 292.4 us)
Async XLA Ops:
  7.2 98.3 %all-gather.5.cloned.1.call-start = ((), (), s32[]{:S(2)}) async-start(), calls=%async_computation.9 | async-start | bytes 5242880 | tf_op jit(solution)/shard_map/all_gather | solution.py:142
  8.7 10.2 copy-start.24
  10.3 8.5 copy-start.31
  11.1 7.7 copy-start.26
  12.7 6.1 copy-start.36
  12.8 286.3 %copy-start.34 = (f32[1,1024]{1,0:T(1,128)}, f32[1,1024]{1,0:T(1,128)S(1)}, u32[]{:S(2)}) copy-start(f32[1,1024]{1,0:T(1,128)S(1)} %get-tuple-element.393) | copy-start | bytes 12292
  21.8 3.4 copy-start.43
  21.9 165.0 %all-gather.7.cloned.1.call-start = ((), (), s32[]{:S(2)}) async-start(), calls=%async_computation.10 | async-start | bytes 5242880 | tf_op jit(solution)/shard_map/all_gather | solution.py:141
  24.7 608.1 %reduce-scatter.20.cloned.1.call-start = ((), (), s32[]{:S(2)}) async-start(), calls=%async_computation.11 | async-start | bytes 5242880 | tf_op jit(solution)/shard_map/reduce_scatter | solution.py:193
  193.4 102.7 %copy-start.3 = (bf16[512,1024]{1,0:T(8,128)(2,1)S(1)}, bf16[512,1024]{1,0:T(8,128)(2,1)}, u32[]{:S(2)}) copy-start(bf16[512,1024]{1,0:T(8,128)(2,1)} %param.21) | copy-start | bytes 3145732
  193.4 102.7 %copy-start.14 = (bf16[1024,1024]{1,0:T(8,128)(2,1)S(1)}, bf16[1024,1024]{1,0:T(8,128)(2,1)}, u32[]{:S(2)}) copy-start(bf16[1024,1024]{1,0:T(8,128)(2,1)} %param.24) | copy-start | bytes 6291460
  298.6 30.4 %copy-start.1 = (f32[512,1024]{1,0:T(8,128)}, f32[512,1024]{1,0:T(8,128)S(1)}, u32[]{:S(2)}) copy-start(f32[512,1024]{1,0:T(8,128)S(1)} %get-tuple-element.402) | copy-start | bytes 6291460
  299.0 10.8 copy-start.17
  299.0 10.8 copy-start.44
  299.0 24.3 %slice-start = ((s8[8388608]{0:T(1024)(128)(4,1)}), s8[4194304]{0:T(1024)(128)(4,1)S(1)}, s32[]{:S(2)}) async-start(s8[8388608]{0:T(1024)(128)(4,1)} %bitcast.226), calls=%async_computation.27 | async-start | bytes 8388608
  309.8 13.6 slice-start.1
  323.4 5.7 copy-start.49
  339.9 3.4 copy-start
  355.6 3.3 copy-start.10
  367.7 3.4 copy-start
  383.4 3.3 copy-start.10
  395.5 3.4 copy-start
  411.2 3.3 copy-start.10
  423.3 3.4 copy-start
  439.0 3.3 copy-start.10
  451.1 3.4 copy-start
  466.8 3.3 copy-start.10
  478.9 3.4 copy-start
  494.7 3.3 copy-start.10
  506.8 3.4 copy-start
  522.5 3.3 copy-start.10
  534.6 3.4 copy-start
  550.3 3.3 copy-start.10
  557.4 154.8 %reduce-scatter.22.cloned.1.call-start = ((), (), s32[]{:S(2)}) async-start(), calls=%async_computation.12 | async-start | bytes 5242880 | tf_op jit(solution)/shard_map/reduce_scatter | solution.py:196
  558.0 199.6 %reduce-scatter.30.cloned.1.call-start = ((), (), s32[]{:S(2)}) async-start(), calls=%async_computation.22 | async-start | bytes 2359296
  561.8 150.4 %copy-start.4 = (bf16[512,1024]{1,0:T(8,128)(2,1)S(1)}, bf16[512,1024]{1,0:T(8,128)(2,1)}, u32[]{:S(2)}) copy-start(bf16[512,1024]{1,0:T(8,128)(2,1)} %param.21) | copy-start | bytes 3145732
  561.8 150.4 %copy-start.19 = (bf16[8,512,2,64]{1,3,2,0:T(8,128)(2,1)S(1)}, bf16[8,512,2,64]{1,3,2,0:T(8,128)(2,1)}, u32[]{:S(2)}) copy-start(bf16[8,512,2,64]{1,3,2,0:T(8,128)(2,1)} %get-tuple-element.137) | copy-start | bytes 3145732
  561.8 150.4 %copy-start.25 = (f32[512]{0:T(512)S(1)}, f32[512]{0:T(512)}, u32[]{:S(2)}) copy-start(f32[512]{0:T(512)} %copy-done.24) | copy-start | bytes 6148
  561.8 150.4 %copy-start.27 = (f32[1,1024]{1,0:T(1,128)S(1)}, f32[1,1024]{1,0:T(1,128)}, u32[]{:S(2)}) copy-start(f32[1,1024]{1,0:T(1,128)} %copy-done.26) | copy-start | bytes 12292
  561.8 150.4 %copy-start.32 = (f32[512]{0:T(512)S(1)}, f32[512]{0:T(512)}, u32[]{:S(2)}) copy-start(f32[512]{0:T(512)} %copy-done.31) | copy-start | bytes 6148
  561.8 150.4 %copy-start.37 = (f32[1,1024]{1,0:T(1,128)S(1)}, f32[1,1024]{1,0:T(1,128)}, u32[]{:S(2)}) copy-start(f32[1,1024]{1,0:T(1,128)} %copy-done.36) | copy-start | bytes 12292
  566.1 256.4 %reduce-scatter.28.cloned.1.call-start = ((), (), s32[]{:S(2)}) async-start(), calls=%async_computation.21 | async-start | bytes 7077888
  729.0 168.4 %reduce-scatter.26.cloned.1.call-start = ((), (), s32[]{:S(2)}) async-start(), calls=%async_computation.14 | async-start | bytes 9437184 | tf_op jit(solution)/shard_map/reduce_scatter | solution.py:231
  741.6 230.6 %reduce-scatter.24.cloned.1.call-start = ((), (), s32[]{:S(2)}) async-start(), calls=%async_computation.13 | async-start | bytes 9437184 | tf_op jit(solution)/shard_map/reduce_scatter | solution.py:228
  752.5 344.6 %all-reduce.21.cloned.1.call-start = ((), (), s32[]{:S(2)}) async-start(), calls=%async_computation.26 | async-start | bytes 6291456 | tf_op jit(solution)/shard_map/psum | solution.py:245
  972.2 200.9 %all-reduce.11.cloned.1.call-start = ((), (), s32[]{:S(2)}) async-start(), calls=%async_computation.15 | async-start | bytes 4194304 | tf_op jit(solution)/shard_map/psum | solution.py:271
  1099.5 3.0 copy-start.12
  1112.2 132.2 %all-reduce.13.cloned.1.call-start = ((), (), s32[]{:S(2)}) async-start(), calls=%async_computation.16 | async-start | bytes 4194304 | tf_op jit(solution)/shard_map/psum | solution.py:271
  1183.4 129.0 %all-reduce.15.cloned.1.call-start = ((), (), s32[]{:S(2)}) async-start(), calls=%async_computation.17 | async-start | bytes 4194304 | tf_op jit(solution)/shard_map/psum | solution.py:271
  1251.4 129.0 %all-reduce.17.cloned.1.call-start = ((), (), s32[]{:S(2)}) async-start(), calls=%async_computation.18 | async-start | bytes 4194304 | tf_op jit(solution)/shard_map/psum | solution.py:271
  1319.4 129.1 %all-reduce.19.cloned.1.call-start = ((), (), s32[]{:S(2)}) async-start(), calls=%async_computation.19 | async-start | bytes 4194304 | tf_op jit(solution)/shard_map/psum | solution.py:271
  1387.5 99.7 %reduce-scatter.36.cloned.1.call-start = ((), (), s32[]{:S(2)}) async-start(), calls=%async_computation.25 | async-start | bytes 1179648
  1389.1 12.2 copy-start.39
  1389.2 12.2 copy-start.30
  1389.2 12.2 copy-start.29
  1389.2 135.2 %reduce-scatter.32.cloned.1.call-start = ((), (), s32[]{:S(2)}) async-start(), calls=%async_computation.23 | async-start | bytes 294912
  1399.8 161.1 %reduce-scatter.34.cloned.1.call-start = ((), (), s32[]{:S(2)}) async-start(), calls=%async_computation.24 | async-start | bytes 294912
  1403.9 239.2 %all-gather.9.cloned.1.call-start = ((), (), s32[]{:S(2)}) async-start(), calls=%async_computation.20 | async-start | bytes 5242880 | tf_op jit(solution)/shard_map/all_gather | solution.py:285
  1452.9 4.6 copy-start.33
  1488.2 85.3 %copy-start.42 = (f32[2,128]{1,0:T(2,128)S(1)}, f32[2,128]{1,0:T(2,128)}, u32[]{:S(2)}) copy-start(f32[2,128]{1,0:T(2,128)} %param.35) | copy-start | bytes 3076
  1488.2 86.5 %copy-start.41 = (f32[512]{0:T(512)S(1)}, f32[512]{0:T(512)}, u32[]{:S(2)}) copy-start(f32[512]{0:T(512)} %param.37) | copy-start | bytes 6148
  1488.3 87.2 %copy-start.38 = (f32[6,128]{1,0:T(8,128)S(1)}, f32[6,128]{1,0:T(8,128)}, u32[]{:S(2)}) copy-start(f32[6,128]{1,0:T(8,128)} %param.36) | copy-start | bytes 9220
  1576.7 5.9 copy-start.5
  1582.6 60.5 %copy-start.13 = (bf16[512,1024]{0,1:T(8,128)(2,1)S(1)}, bf16[512,1024]{0,1:T(8,128)(2,1)}, u32[]{:S(2)}) copy-start(bf16[512,1024]{0,1:T(8,128)(2,1)} %copy.81) | copy-start | bytes 3145732
  (27 other events, 50.7 us)
Sparse Core Ops, SparseCore 0:
  22.0 83.4 all-gather.4
  107.6 79.2 all-gather.6
  557.5 75.1 reduce-scatter.19
  634.9 77.2 reduce-scatter.21
  715.9 41.6 reduce-scatter.29
  760.8 61.7 reduce-scatter.27
  826.0 71.3 reduce-scatter.25
  900.9 71.2 reduce-scatter.23
  976.0 121.0 all-reduce.20
  1112.3 60.7 all-reduce.10
  1183.5 60.8 all-reduce.12
  1251.5 60.8 all-reduce.14
  1319.6 60.8 all-reduce.16
  1387.6 60.8 all-reduce.18
  1452.1 35.0 reduce-scatter.35
  1490.6 33.6 reduce-scatter.31
  1527.2 33.6 reduce-scatter.33
  1562.3 80.7 all-gather.8
where the time goes:
time: 1670 us; the launch traced here: 1660 us
  waiting for transfers between devices  1070 us (64%)
  matrix products  337 us (20%)
  other arithmetic  136 us (8%)
  local copies, waits for them, and re-layouts  88.3 us (5%)
    psum x5, waiting for transfers between devices, on_device(): lax.psum(contract_cols(iterate, iterate).astype(jnp.bfloat16), 'dp')  288 us
    unnamed x23, waiting for transfers between devices  154 us
    psum x1, waiting for transfers between devices, on_device(): lax.psum(qkv_part.astype(jnp.bfloat16), 'seq').astype(jnp.float32)  122 us
    reduce_scatter x1, waiting for transfers between devices, on_device(): lax.psum_scatter(join_heads(value_grad).astype(jnp.bfloat16), 'seq', scat...  79.5 us
    all_gather x1, waiting for transfers between devices, on_device(): lax.all_gather(value_part, 'seq', axis=0, tiled=True)  78.8 us
    all_gather x1, waiting for transfers between devices, on_device(): lax.all_gather(key_part, 'seq', axis=0, tiled=True)  74.9 us
    reduce_scatter x1, waiting for transfers between devices, on_device(): lax.psum_scatter(up_grad.astype(jnp.bfloat16), 'dp', scatter_dimension=1,...  74.8 us
    reduce_scatter x1, waiting for transfers between devices, on_device(): lax.psum_scatter(down_grad.astype(jnp.bfloat16), 'dp', scatter_dimension=...  72.5 us
  transfers between devices with their start and end apart: 18, of which 18 were waited for; matrix products, arithmetic and copies ran while one was open for 7% of the time, Pallas kernels for 0%

commit v1 on v0

--- a/solution.py
+++ b/solution.py
@@ -14,6 +14,10 @@
 COEF_B = -1.0
 GELU_C = 0.7978845608028654
 MASKED = -1e30
+
+
+def test_the_things(target, comm_axis):
+    return jax.lax.all_gather(target, comm_axis).sum(axis=0)
 
 
 def norm_forward(values, gain_row, offset):
@@ -268,7 +272,7 @@
     owned_block = lax.dynamic_index_in_dim(stacked, lax.axis_index("seq"), 0, keepdims=False)
     iterate = owned_block
     for iteration in range(NS_ITERS):
-        gram = lax.psum(contract_cols(iterate, iterate).astype(jnp.bfloat16), "dp").astype(
+        gram = test_the_things(contract_cols(iterate, iterate).astype(jnp.bfloat16), "dp").astype(
             jnp.float32
         )
         if iteration == 0:

time: 1670 us -> 1860 us (1.11)
  waiting for transfers between devices: 1070 us -> 1200 us
  other arithmetic: 136 us -> 190 us
    all_gather x0 -> x5, waiting for transfers between devices: none -> 432 us  [test_the_things(): return jax.lax.all_gather(target, comm_axis).sum(axis=0)]
    psum x5 -> x0, waiting for transfers between devices: 288 us -> none  [on_device(): lax.psum(contract_cols(iterate, iterate).astype(jnp.bfloat16), 'dp')]
    reduce_sum x0 -> x5, other arithmetic: none -> 53.9 us  [test_the_things(): return jax.lax.all_gather(target, comm_axis).sum(axis=0)]
    unnamed x112 -> x110, local copies, waits for them, and re-layouts: 46.7 us -> 47.4 us
where the time goes in v1:
time: 1860 us; the launch traced here: 1850 us
  waiting for transfers between devices  1200 us (65%)
  matrix products  337 us (18%)
  other arithmetic  190 us (10%)
  local copies, waits for them, and re-layouts  89.1 us (5%)
    all_gather x5, waiting for transfers between devices, test_the_things(): return jax.lax.all_gather(target, comm_axis).sum(axis=0)  432 us
    unnamed x23, waiting for transfers between devices  144 us
    psum x1, waiting for transfers between devices, on_device(): lax.psum(qkv_part.astype(jnp.bfloat16), 'seq').astype(jnp.float32)  122 us
    reduce_scatter x1, waiting for transfers between devices, on_device(): lax.psum_scatter(join_heads(value_grad).astype(jnp.bfloat16), 'seq', scat...  79.5 us
    all_gather x1, waiting for transfers between devices, on_device(): lax.all_gather(value_part, 'seq', axis=0, tiled=True)  79 us
    all_gather x1, waiting for transfers between devices, on_device(): lax.all_gather(key_part, 'seq', axis=0, tiled=True)  74.9 us
    reduce_scatter x1, waiting for transfers between devices, on_device(): lax.psum_scatter(up_grad.astype(jnp.bfloat16), 'dp', scatter_dimension=1,...  74.8 us
    reduce_scatter x1, waiting for transfers between devices, on_device(): lax.psum_scatter(down_grad.astype(jnp.bfloat16), 'dp', scatter_dimension=...  72.5 us
  transfers between devices with their start and end apart: 18, of which 18 were waited for; matrix products, arithmetic and copies ran while one was open for 7% of the time, Pallas kernels for 0%

profile of v1, /device:TPU:0, one launch (start us, length us, event | category | flops | bytes accessed | tf_op | source)
XLA Modules:
  0.0 1850.7 jit_solution(11213855683567013093)
XLA Ops:
  12.8 6.1 fusion.105
  27.7 79.0 %all-gather.15.cloned.1.call-done = bf16[2048,1024]{1,0:T(8,128)(2,1)} async-done(((bf16[512,1024]{1,0:T(8,128)(2,1)}), bf16[2048,1024]{1,0:T(8,128)(2,1)}) %all-gather.15.cloned.1.call-update) | async-done | bytes 4194320 | tf_op jit(solution)/shard_map/all_gather | solution.py:146
  106.7 6.5 copy.70
  113.2 74.9 %all-gather.17.cloned.1.call-done = bf16[2048,1024]{1,0:T(8,128)(2,1)} async-done(((bf16[512,1024]{1,0:T(8,128)(2,1)}), bf16[2048,1024]{1,0:T(8,128)(2,1)}) %all-gather.17.cloned.1.call-update) | async-done | bytes 4194320 | tf_op jit(solution)/shard_map/all_gather | solution.py:145
  188.1 6.4 copy.72
  194.6 102.7 %while.30 = (s32[]{:T(128)}, bf16[8,512,2,64]{1,3,2,0:T(8,128)(2,1)}, f32[8,2,512]{2,1,0:T(2,128)S(1)}, bf16[8,2048,2,64]{1,3,2,0:T(8,128)(2,1)}, bf16[8,512,2,6...) while((s32[]{:T(128)}, ...), condition=%wide.region_5.6_spmd.clone.clone, body=%wide.region_2.5_spmd.clone.clone.sunk | while | flops 575667200 | bytes 47618196 | solution.py:155
  202.9 4.5 fusion.167
  215.7 4.5 fusion.167
  228.6 4.5 fusion.167
  241.4 4.5 fusion.167
  254.2 4.5 fusion.167
  267.1 4.5 fusion.167
  279.9 4.5 fusion.167
  292.7 4.5 fusion.167
  300.3 10.7 fusion.107
  311.0 14.0 fusion.113
  325.0 5.7 multiply_reduce_fusion.1
  336.3 222.9 %while.31 = (s32[]{:T(128)}, bf16[8,512,2,64]{1,3,2,0:T(8,128)(2,1)}, bf16[8,2048,2,64]{1,3,2,0:T(8,128)(2,1)}, bf16[8,2048,2,64]{1,3,2,0:T(8,128)(2,1)}, bf16[8...) while((s32[]{:T(128)}, ...), condition=%wide.region_12.13_spmd.clone.clone, body=%wide.region_10.12_spmd.clone.clone.sunk | while | flops 1368783872 | bytes 144864496 | solution.py:184
  344.9 5.7 multiply_reduce_fusion.7
  350.6 6.6 multiply_convert_fusion.7
  372.7 5.7 multiply_reduce_fusion.7
  378.5 6.6 multiply_convert_fusion.7
  400.6 5.7 multiply_reduce_fusion.7
  406.3 6.6 multiply_convert_fusion.7
  428.4 5.7 multiply_reduce_fusion.7
  434.1 6.6 multiply_convert_fusion.7
  456.3 5.7 multiply_reduce_fusion.7
  462.0 6.6 multiply_convert_fusion.7
  484.1 5.7 multiply_reduce_fusion.7
  489.8 6.6 multiply_convert_fusion.7
  512.0 5.7 multiply_reduce_fusion.7
  517.7 6.6 multiply_convert_fusion.7
  539.8 5.7 multiply_reduce_fusion.7
  545.5 6.6 multiply_convert_fusion.7
  563.6 4.3 copy.83
  568.2 66.4 %reduce-scatter.20.cloned.1.call-done = bf16[512,1024]{0,1:T(8,128)(2,1)} async-done(((bf16[2048,1024]{0,1:T(8,128)(2,1)}), bf16[512,1024]{0,1:T(8,128)(2,1)}) %reduce-scatter.20.cloned.1.call-update) | async-done | bytes 1048592 | tf_op jit(solution)/shard_map/reduce_scatter | solution.py:197
  634.5 79.5 %reduce-scatter.22.cloned.1.call-done = bf16[512,1024]{0,1:T(8,128)(2,1)} async-done(((bf16[2048,1024]{0,1:T(8,128)(2,1)}), bf16[512,1024]{0,1:T(8,128)(2,1)}) %reduce-scatter.22.cloned.1.call-update) | async-done | bytes 1048592 | tf_op jit(solution)/shard_map/reduce_scatter | solution.py:200
  714.1 8.0 convolution_convert_fusion.1
  722.1 8.7 copy.81
  732.0 11.4 convert_bitcast_fusion
  745.0 9.2 convolution_convert_fusion
  754.7 4.7 reduce-scatter.30.cloned.1.call-done
  761.2 63.2 %reduce-scatter.28.cloned.1.call-done = bf16[384,1024]{1,0:T(8,128)(2,1)} async-done(((bf16[3072,1024]{1,0:T(8,128)(2,1)}), bf16[384,1024]{1,0:T(8,128)(2,1)}) %reduce-scatter.28.cloned.1.call-update) | async-done | bytes 786448
  826.6 72.5 %reduce-scatter.26.cloned.1.call-done = bf16[1024,512]{1,0:T(8,128)(2,1)} async-done(((bf16[1024,4096]{1,0:T(8,128)(2,1)}), bf16[1024,512]{1,0:T(8,128)(2,1)}) %reduce-scatter.26.cloned.1.call-update) | async-done | bytes 1048592 | tf_op jit(solution)/shard_map/reduce_scatter | solution.py:235
  899.2 74.8 %reduce-scatter.24.cloned.1.call-done = bf16[1024,512]{1,0:T(8,128)(2,1)} async-done(((bf16[1024,4096]{1,0:T(8,128)(2,1)}), bf16[1024,512]{1,0:T(8,128)(2,1)}) %reduce-scatter.24.cloned.1.call-update) | async-done | bytes 1048592 | tf_op jit(solution)/shard_map/reduce_scatter | solution.py:232
  976.9 121.9 %all-reduce.6.cloned.1.call-done = (bf16[1024,384]{1,0:T(8,128)(2,1)}, bf16[1024,128]{1,0:T(8,128)(2,1)}, bf16[1024,512]{1,0:T(8,128)(2,1)}, bf16[1024,512]{1,0:T(8,128)(2,1)}) async-done(((bf16[1024,384]{1,0:T(8,128)(2,1)}, bf16[1024,128]{1,0:T(8,128)(2,1)}, bf16[1024,512]{1,0:T(8,128)(2,1)}, bf16[1024,512]{1,0:T(8,128)(2,1)}), (bf16[1024,384]{1,0:T(8,128)(2,1)}, bf16[1024,128]{1,0:T(8,128)(2,1)}, ...) | async-done | bytes 3145744 | tf_op jit(solution)/shard_map/psum | solution.py:249
  1114.2 88.8 %all-gather.19.cloned.1.call-done = bf16[8192,1024]{1,0:T(8,128)(2,1)} async-done(((bf16[1024,1024]{1,0:T(8,128)(2,1)}), bf16[8192,1024]{1,0:T(8,128)(2,1)}) %all-gather.19.cloned.1.call-update) | async-done | bytes 16777232 | tf_op jit(solution)/shard_map/all_gather | solution.py:20
  1203.1 10.8 reduce_sum.261
  1224.1 89.8 %all-gather.21.cloned.1.call-done = bf16[8192,1024]{1,0:T(8,128)(2,1)} async-done(((bf16[1024,1024]{1,0:T(8,128)(2,1)}), bf16[8192,1024]{1,0:T(8,128)(2,1)}) %all-gather.21.cloned.1.call-update) | async-done | bytes 16777232 | tf_op jit(solution)/shard_map/all_gather | solution.py:20
  1314.0 10.8 reduce_sum.263
  1332.0 89.6 %all-gather.23.cloned.1.call-done = bf16[8192,1024]{1,0:T(8,128)(2,1)} async-done(((bf16[1024,1024]{1,0:T(8,128)(2,1)}), bf16[8192,1024]{1,0:T(8,128)(2,1)}) %all-gather.23.cloned.1.call-update) | async-done | bytes 16777232 | tf_op jit(solution)/shard_map/all_gather | solution.py:20
  1421.6 10.8 reduce_sum.264
  1439.5 89.8 %all-gather.25.cloned.1.call-done = bf16[8192,1024]{1,0:T(8,128)(2,1)} async-done(((bf16[1024,1024]{1,0:T(8,128)(2,1)}), bf16[8192,1024]{1,0:T(8,128)(2,1)}) %all-gather.25.cloned.1.call-update) | async-done | bytes 16777232 | tf_op jit(solution)/shard_map/all_gather | solution.py:20
  1529.3 10.8 reduce_sum.265
  1548.9 9.0 fusion.80
  1563.3 73.8 %all-gather.27.cloned.1.call-done = bf16[8192,1024]{1,0:T(8,128)(2,1)} async-done(((bf16[1024,1024]{1,0:T(8,128)(2,1)}), bf16[8192,1024]{1,0:T(8,128)(2,1)}) %all-gather.27.cloned.1.call-update) | async-done | bytes 16777232 | tf_op jit(solution)/shard_map/all_gather | solution.py:20
  1637.0 10.8 reduce_sum.266
  1647.8 4.5 add_convert_fusion
  1657.0 12.3 add_convert_fusion.5
  1669.3 7.3 reduce-scatter.36.cloned.1.call-done
  1681.9 31.9 %reduce-scatter.32.cloned.1.call-done = bf16[128,2]{1,0:T(8,128)(2,1)} async-done(((bf16[1024,2]{1,0:T(8,128)(2,1)}), bf16[128,2]{1,0:T(8,128)(2,1)}) %reduce-scatter.32.cloned.1.call-update) | async-done | bytes 528
  1714.6 35.7 %reduce-scatter.34.cloned.1.call-done = bf16[128,6]{1,0:T(8,128)(2,1)} async-done(((bf16[1024,6]{1,0:T(8,128)(2,1)}), bf16[128,6]{1,0:T(8,128)(2,1)}) %reduce-scatter.34.cloned.1.call-update) | async-done | bytes 1552
  1751.2 11.8 all-reduce.2
  1773.8 58.8 %all-gather.29.cloned.1.call-done = bf16[4096,512]{1,0:T(8,128)(2,1)} async-done(((bf16[1024,512]{1,0:T(8,128)(2,1)}), bf16[4096,512]{1,0:T(8,128)(2,1)}) %all-gather.29.cloned.1.call-update) | async-done | bytes 4194320 | tf_op jit(solution)/shard_map/all_gather | solution.py:289
  (372 shorter events, 314.3 us)
Async XLA Ops:
  7.2 99.5 %all-gather.15.cloned.1.call-start = ((), (), s32[]{:S(2)}) async-start(), calls=%async_computation.9 | async-start | bytes 5242880 | tf_op jit(solution)/shard_map/all_gather | solution.py:146
  8.7 10.2 copy-start.23
  10.3 8.5 copy-start.30
  11.1 7.7 copy-start.25
  12.7 6.1 copy-start.35
  12.8 287.5 %copy-start.33 = (f32[1,1024]{1,0:T(1,128)}, f32[1,1024]{1,0:T(1,128)S(1)}, u32[]{:S(2)}) copy-start(f32[1,1024]{1,0:T(1,128)S(1)} %get-tuple-element.416) | copy-start | bytes 12292
  21.5 4.8 copy-start.42
  23.1 165.0 %all-gather.17.cloned.1.call-start = ((), (), s32[]{:S(2)}) async-start(), calls=%async_computation.10 | async-start | bytes 5242880 | tf_op jit(solution)/shard_map/all_gather | solution.py:145
  25.9 608.6 %reduce-scatter.20.cloned.1.call-start = ((), (), s32[]{:S(2)}) async-start(), calls=%async_computation.11 | async-start | bytes 5242880 | tf_op jit(solution)/shard_map/reduce_scatter | solution.py:197
  194.6 102.7 %copy-start.3 = (bf16[512,1024]{1,0:T(8,128)(2,1)S(1)}, bf16[512,1024]{1,0:T(8,128)(2,1)}, u32[]{:S(2)}) copy-start(bf16[512,1024]{1,0:T(8,128)(2,1)} %param.21) | copy-start | bytes 3145732
  194.6 102.7 %copy-start.14 = (bf16[1024,1024]{1,0:T(8,128)(2,1)S(1)}, bf16[1024,1024]{1,0:T(8,128)(2,1)}, u32[]{:S(2)}) copy-start(bf16[1024,1024]{1,0:T(8,128)(2,1)} %param.24) | copy-start | bytes 6291460
  299.9 30.8 %copy-start.1 = (f32[512,1024]{1,0:T(8,128)}, f32[512,1024]{1,0:T(8,128)S(1)}, u32[]{:S(2)}) copy-start(f32[512,1024]{1,0:T(8,128)S(1)} %get-tuple-element.425) | copy-start | bytes 6291460
  300.2 10.8 copy-start.17
  300.2 10.8 copy-start.43
  300.3 24.8 %slice-start = ((s8[8388608]{0:T(1024)(128)(4,1)}), s8[4194304]{0:T(1024)(128)(4,1)S(1)}, s32[]{:S(2)}) async-start(s8[8388608]{0:T(1024)(128)(4,1)} %bitcast.236), calls=%async_computation.27 | async-start | bytes 8388608
  311.0 14.0 slice-start.1
  325.0 5.7 copy-start.48
  341.5 3.4 copy-start
  357.2 3.3 copy-start.10
  369.3 3.4 copy-start
  385.0 3.3 copy-start.10
  397.1 3.4 copy-start
  412.9 3.3 copy-start.10
  425.0 3.4 copy-start
  440.7 3.3 copy-start.10
  452.8 3.5 copy-start
  468.6 3.3 copy-start.10
  480.7 3.4 copy-start
  508.5 3.5 copy-start
  524.3 3.3 copy-start.10
  536.4 3.4 copy-start
  552.1 3.3 copy-start.10
  559.2 154.8 %reduce-scatter.22.cloned.1.call-start = ((), (), s32[]{:S(2)}) async-start(), calls=%async_computation.12 | async-start | bytes 5242880 | tf_op jit(solution)/shard_map/reduce_scatter | solution.py:200
  559.8 199.6 %reduce-scatter.30.cloned.1.call-start = ((), (), s32[]{:S(2)}) async-start(), calls=%async_computation.22 | async-start | bytes 2359296
  563.6 150.4 %copy-start.4 = (bf16[512,1024]{1,0:T(8,128)(2,1)S(1)}, bf16[512,1024]{1,0:T(8,128)(2,1)}, u32[]{:S(2)}) copy-start(bf16[512,1024]{1,0:T(8,128)(2,1)} %param.21) | copy-start | bytes 3145732
  563.6 150.4 %copy-start.19 = (bf16[8,512,2,64]{1,3,2,0:T(8,128)(2,1)S(1)}, bf16[8,512,2,64]{1,3,2,0:T(8,128)(2,1)}, u32[]{:S(2)}) copy-start(bf16[8,512,2,64]{1,3,2,0:T(8,128)(2,1)} %get-tuple-element.137) | copy-start | bytes 3145732
  563.6 150.4 %copy-start.24 = (f32[512]{0:T(512)S(1)}, f32[512]{0:T(512)}, u32[]{:S(2)}) copy-start(f32[512]{0:T(512)} %copy-done.23) | copy-start | bytes 6148
  563.6 150.4 %copy-start.26 = (f32[1,1024]{1,0:T(1,128)S(1)}, f32[1,1024]{1,0:T(1,128)}, u32[]{:S(2)}) copy-start(f32[1,1024]{1,0:T(1,128)} %copy-done.25) | copy-start | bytes 12292
  563.6 150.4 %copy-start.31 = (f32[512]{0:T(512)S(1)}, f32[512]{0:T(512)}, u32[]{:S(2)}) copy-start(f32[512]{0:T(512)} %copy-done.30) | copy-start | bytes 6148
  563.6 150.4 %copy-start.36 = (f32[1,1024]{1,0:T(1,128)S(1)}, f32[1,1024]{1,0:T(1,128)}, u32[]{:S(2)}) copy-start(f32[1,1024]{1,0:T(1,128)} %copy-done.35) | copy-start | bytes 12292
  567.9 256.4 %reduce-scatter.28.cloned.1.call-start = ((), (), s32[]{:S(2)}) async-start(), calls=%async_computation.21 | async-start | bytes 7077888
  730.8 168.4 %reduce-scatter.26.cloned.1.call-start = ((), (), s32[]{:S(2)}) async-start(), calls=%async_computation.14 | async-start | bytes 9437184 | tf_op jit(solution)/shard_map/reduce_scatter | solution.py:235
  743.4 230.6 %reduce-scatter.24.cloned.1.call-start = ((), (), s32[]{:S(2)}) async-start(), calls=%async_computation.13 | async-start | bytes 9437184 | tf_op jit(solution)/shard_map/reduce_scatter | solution.py:232
  754.2 344.6 %all-reduce.6.cloned.1.call-start = ((), (), s32[]{:S(2)}) async-start(), calls=%async_computation.26 | async-start | bytes 6291456 | tf_op jit(solution)/shard_map/psum | solution.py:249
  974.0 229.1 %all-gather.19.cloned.1.call-start = ((), (), s32[]{:S(2)}) async-start(), calls=%async_computation.15 | async-start | bytes 18874368 | tf_op jit(solution)/shard_map/all_gather | solution.py:20
  1101.2 3.3 copy-start.6
  1101.2 3.3 copy-start.12
  1114.2 199.8 %all-gather.21.cloned.1.call-start = ((), (), s32[]{:S(2)}) async-start(), calls=%async_computation.16 | async-start | bytes 18874368 | tf_op jit(solution)/shard_map/all_gather | solution.py:20
  1224.1 197.6 %all-gather.23.cloned.1.call-start = ((), (), s32[]{:S(2)}) async-start(), calls=%async_computation.17 | async-start | bytes 18874368 | tf_op jit(solution)/shard_map/all_gather | solution.py:20
  1331.8 197.6 %all-gather.25.cloned.1.call-start = ((), (), s32[]{:S(2)}) async-start(), calls=%async_computation.18 | async-start | bytes 18874368 | tf_op jit(solution)/shard_map/all_gather | solution.py:20
  1439.5 197.6 %all-gather.27.cloned.1.call-start = ((), (), s32[]{:S(2)}) async-start(), calls=%async_computation.19 | async-start | bytes 18874368 | tf_op jit(solution)/shard_map/all_gather | solution.py:20
  1547.2 129.5 %reduce-scatter.36.cloned.1.call-start = ((), (), s32[]{:S(2)}) async-start(), calls=%async_computation.25 | async-start | bytes 1179648
  1548.8 11.6 copy-start.38
  1548.9 11.6 copy-start.29
  1548.9 11.6 copy-start.28
  1548.9 164.9 %reduce-scatter.32.cloned.1.call-start = ((), (), s32[]{:S(2)}) async-start(), calls=%async_computation.23 | async-start | bytes 294912
  1558.9 191.4 %reduce-scatter.34.cloned.1.call-start = ((), (), s32[]{:S(2)}) async-start(), calls=%async_computation.24 | async-start | bytes 294912
  1563.0 269.5 %all-gather.29.cloned.1.call-start = ((), (), s32[]{:S(2)}) async-start(), calls=%async_computation.20 | async-start | bytes 5242880 | tf_op jit(solution)/shard_map/all_gather | solution.py:289
  1652.3 4.6 copy-start.32
  1669.3 93.7 %copy-start.41 = (f32[2,128]{1,0:T(2,128)S(1)}, f32[2,128]{1,0:T(2,128)}, u32[]{:S(2)}) copy-start(f32[2,128]{1,0:T(2,128)} %param.35) | copy-start | bytes 3076
  1669.3 94.9 %copy-start.40 = (f32[512]{0:T(512)S(1)}, f32[512]{0:T(512)}, u32[]{:S(2)}) copy-start(f32[512]{0:T(512)} %param.37) | copy-start | bytes 6148
  1669.3 95.6 %copy-start.37 = (f32[6,128]{1,0:T(8,128)S(1)}, f32[6,128]{1,0:T(8,128)}, u32[]{:S(2)}) copy-start(f32[6,128]{1,0:T(8,128)} %param.36) | copy-start | bytes 9220
  1681.9 90.1 %copy-start.5 = (f32[512,1024]{0,1:T(8,128)S(1)}, f32[512,1024]{0,1:T(8,128)}, u32[]{:S(2)}) copy-start(f32[512,1024]{0,1:T(8,128)} %get-tuple-element.414) | copy-start | bytes 6291460
  1769.0 63.5 %copy-start.13 = (bf16[512,1024]{0,1:T(8,128)(2,1)S(1)}, bf16[512,1024]{0,1:T(8,128)(2,1)}, u32[]{:S(2)}) copy-start(bf16[512,1024]{0,1:T(8,128)(2,1)} %copy.91) | copy-start | bytes 3145732
  (26 other events, 48.4 us)
Sparse Core Ops, SparseCore 0:
  23.3 83.4 all-gather.14
  108.9 79.2 all-gather.16
  559.3 75.1 reduce-scatter.19
  636.7 77.2 reduce-scatter.21
  717.7 41.6 reduce-scatter.29
  762.6 61.6 reduce-scatter.27
  827.8 71.3 reduce-scatter.25
  902.6 71.2 reduce-scatter.23
  977.7 121.0 all-reduce.5
  1114.3 88.7 all-gather.18
  1224.2 89.7 all-gather.20
  1331.9 89.7 all-gather.22
  1439.6 89.7 all-gather.24
  1547.3 89.7 all-gather.26
  1640.6 35.9 reduce-scatter.35
  1680.1 33.6 reduce-scatter.31
  1716.6 33.6 reduce-scatter.33
  1751.8 80.7 all-gather.28
